TPU v7x, 8 devices: a whole 2x2x1 slice. The times are simulated.
8 devices in a mesh: dp: 1 (over z), tp: 2 (over y), ep: 4 (over x, core).
Axes of the slice: x: 2, y: 2, z: 1, core: 2. Of those that a mesh axis runs over, the one named last changes fastest.
Arguments:
- hidden_in: bfloat16 [32, 256, 768], P(('dp', 'ep'), 'tp')
- ln_attn: float32 [2, 768], replicated
- ln_ffn: float32 [2, 768], replicated
- w_query: bfloat16 [2, 768, 768], P(None, None, 'tp')
- w_key: bfloat16 [2, 768, 768], P(None, None, 'tp')
- w_value: bfloat16 [2, 768, 768], P(None, None, 'tp')
- w_out: bfloat16 [2, 768, 768], P(None, 'tp')
- bias_table: float32 [2, 12, 32], P(None, 'tp')
- w_gate: bfloat16 [768, 3072], P(None, 'tp')
- w_up: bfloat16 [768, 3072], P(None, 'tp')
- w_down: bfloat16 [3072, 768], P('tp')
- w_router: float32 [768, 64], replicated
- expert_in: bfloat16 [64, 768, 3072], P(('tp', 'ep'))
- expert_out: bfloat16 [64, 3072, 768], P(('tp', 'ep'))
- expert_ids: int32 [32, 256, 2], P(('dp', 'ep'), 'tp')
Outputs:
- output 1: bfloat16 [32, 256, 768], P(('dp', 'ep'), 'tp')
- output 2: bfloat16 [2, 32, 12, 256, 64], P(None, ('dp', 'ep'), 'tp')
- output 3: bfloat16 [2, 32, 12, 256, 64], P(None, ('dp', 'ep'), 'tp')
All inputs are finite; a program needn't handle non-finite values.
Results may differ from a plain program's by a relative error of at most 0.0120267.
Values are sent between devices in bfloat16 or wider.
A program may use at most 1 GiB of HBM per device.

v0:
```python
import jax
import jax.numpy as jnp
from jax import lax
from jax.experimental import pallas as pl
from jax.experimental.pallas import tpu as pltpu
from jax.sharding import PartitionSpec as P

EXACT_BUCKETS = 16
THRESHOLDS = (18, 20, 23, 26, 30, 34, 39, 45, 51, 58, 66, 76, 86, 98, 112)
EPSILON = 1e-6
BF16 = jnp.bfloat16
F32 = jnp.float32

def bucket_hot(buckets, seq_len):
    k = lax.broadcasted_iota(jnp.int32, (buckets, seq_len), 1)
    rel = jnp.where(k == 0, 0, seq_len - k)
    bucket = jnp.minimum(rel, EXACT_BUCKETS)
    for threshold in THRESHOLDS:
        bucket = bucket + jnp.where(rel >= threshold, 1, 0)
    return jnp.where(bucket == lax.broadcasted_iota(jnp.int32, (buckets, seq_len), 0), 1.0, 0.0)


MESH = pl.DeviceIdType.MESH
HEADS = 6
NQ = 192
NO = 96
NF = 128
FC = 512
WINDOW = 5
HERE, THERE = range(2)
SELF, CORE, ACROSS, CORNER = range(4)
LOCAL_EXPERTS = 8
CAPACITY = 64


def swap_targets():
    tp = lax.axis_index('tp')
    ep = lax.axis_index('ep')
    core = ep + 1 - 2 * lax.rem(ep, 2)
    across = lax.rem(ep + 2, 4)
    return tp, ep, {'tp': 1 - tp}, {'ep': across}, {'ep': core}


def greet(targets):
    barrier = pltpu.get_barrier_semaphore()
    for target in targets:
        pl.semaphore_signal(barrier, inc=1, device_id=target, device_id_type=MESH)
    pl.semaphore_wait(barrier, len(targets))


def attend_rows(qkv_ref, bias_ref, base, o_ref, side, s):
    width = HEADS * 64
    rows = 128
    lane = lax.broadcasted_iota(jnp.int32, (rows, 128), 1)
    units = [(pair, blk, sd) for pair in range(HEADS // 2) for blk in range(2) for sd in range(2)]
    scores = []
    for pair, blk, sd in units:
        lo = pair * 128
        keys = rows * (blk + 1)
        q = qkv_ref[blk * rows:(blk + 1) * rows, lo:lo + 128]
        k = qkv_ref[0:keys, width + lo:width + lo + 128]
        mine = (lane < 64) if sd == 0 else (lane >= 64)
        qh = jnp.where(mine, q, jnp.zeros_like(q))
        sc = lax.dot_general(qh, k, (((1,), (1,)), ((), ())), preferred_element_type=F32)
        scores.append(sc * 0.125 + bias_ref[base + 2 * pair + sd, blk * rows:(blk + 1) * rows, 0:keys])
    tops = [jnp.max(sc, axis=1, keepdims=True) for sc in scores]
    exps = [jnp.exp(sc - m) for sc, m in zip(scores, tops)]
    sums = [jnp.sum(p, axis=1, keepdims=True) for p in exps]
    probs = [(p * (1.0 / l)).astype(BF16) for p, l in zip(exps, sums)]
    outs = []
    for (pair, blk, sd), p in zip(units, probs):
        lo = pair * 128
        v = qkv_ref[0:rows * (blk + 1), 2 * width + lo:2 * width + lo + 128]
        outs.append(jnp.dot(p, v, preferred_element_type=F32))
    for i in range(0, len(units), 2):
        pair, blk, _ = units[i]
        o_ref[side, s, blk * rows:(blk + 1) * rows, pair * 128:pair * 128 + 128] = jnp.where(
            lane < 64, outs[i], outs[i + 1]).astype(BF16)


def dense_kernel(hid, lna, lnf, wq, wk, wv, wo, wg, wu, wd, table_own, ids, w_router,
                 rows_out, aux, own_h, kc, vc,
                 own_qkv, own_o, own_g, own_u, peer_qkv, peer_o, peer_g, peer_u, pool,
                 table_peer, bias, qkv, o_all, b_all, acc, kvt, other, kvp_ref, h_all, slots_all, ids_row,
                 ysend, yrecv, xsend, xrecv, csend, crecv, dsend, drecv, hsend, hrecv, lsem, osem,
                 asend, arecv, ssend, srecv, ksend, krecv):
    tp, ep, to_y, to_x, to_c = swap_targets()
    eps = [ep, to_c['ep'], to_x['ep'], lax.rem(to_c['ep'] + 2, 4)]
    tps = [tp, 1 - tp]
    me = tp * 4 + ep
    away = [(i, j) for i in (1, 0) for j in (2, 3, 0, 1) if (i, j) != (0, 0)]
    n_exp, capacity = LOCAL_EXPERTS, CAPACITY
    local_slots = n_exp * capacity

    def target(i, j):
        return {'tp': tps[i], 'ep': eps[j]}

    across = lax.rem(ep + 2, 4)
    x_ref = h_all.at[0]
    _, hb, seq, d_model = h_all.shape
    half = seq // 2
    tokens = hb * seq
    width = HEADS * 64
    ff = wd.shape[0]

    attn = [[('w', l, m) for m in range(3)] + [('o', l, 0)] for l in range(2)]
    ffn = [[(kind, c, 0) for kind in ('g', 'u', 'd')] for c in range(3)]
    items = attn[0] + ffn[0] + ffn[1] + ffn[2] + attn[1]
    index = {item: i for i, item in enumerate(items)}

    def source(item):
        kind, l, m = item
        if kind == 'w':
            return (wq, wk, wv)[m].at[l, pl.ds(pl.multiple_of(ep * NQ, NQ), NQ), :]
        if kind == 'o':
            return wo.at[l, pl.ds(pl.multiple_of(ep * NO, NO), NO), :]
        at = pl.multiple_of(ep * (3 * NF) + l * NF, NF)
        if kind == 'd':
            return wd.at[pl.ds(at, NF), :]
        return (wg if kind == 'g' else wu).at[:, pl.ds(at, NF)]

    def place(item, r):
        kind, l, m = item
        if kind == 'w':
            return peer_qkv.at[l, m, pl.ds(pl.multiple_of(r * NQ, NQ), NQ), :]
        if kind == 'o':
            return peer_o.at[l, pl.ds(pl.multiple_of(r * NO, NO), NO), :]
        at = pl.multiple_of(r * NF, NF)
        if kind == 'd':
            return pool.at[pl.ds(pl.multiple_of(ff + l * FC + at, NF), NF), :]
        return (peer_g if kind == 'g' else peer_u).at[l, :, pl.ds(at, NF)]

    def remote(src, dst, send, recv, target):
        return pltpu.make_async_remote_copy(src_ref=src, dst_ref=dst, send_sem=send, recv_sem=recv,
                                            device_id=target, device_id_type=MESH)

    def y_copy(item):
        i = index[item]
        return remote(source(item), place(item, ep), ysend.at[i], yrecv.at[i], to_y)

    def x_copy(item):
        i = index[item]
        return remote(place(item, ep), place(item, ep), xsend.at[i], xrecv.at[i], to_x)

    def c_copy(item):
        i = index[item]
        return remote(place(item, ep), place(item, ep), csend.at[i], crecv.at[i], to_c)

    def d_copy(item):
        i = index[item]
        return remote(place(item, across), place(item, across), dsend.at[i], drecv.at[i], to_c)

    def pass_on(*names):
        for item in names:
            y_copy(item).wait_recv()
            if index[item] + WINDOW < len(sends):
                sends[index[item] + WINDOW].start()
            x_copy(item).start()
            c_copy(item).start()

    def pass_core(*names):
        for item in names:
            x_copy(item).wait_recv()
            d_copy(item).start()

    def complete(*names):
        for item in names:
            c_copy(item).wait_recv()
            d_copy(item).wait_recv()

    mine_at = pl.ds(tp * hb, hb)
    peer_at = pl.ds((1 - tp) * hb, hb)
    rows_at = pl.ds(pl.multiple_of(tp * half, half), half)
    hid_a = remote(hid.at[peer_at], x_ref.at[:, rows_at, :], hsend.at[0], hrecv.at[0], to_y)
    hid_b = remote(hid.at[mine_at], other.at[:, rows_at, :], hsend.at[1], hrecv.at[1], to_y)
    sends = [y_copy(item) for item in items] + [hid_b]
    u_copy = remote(table_own, table_peer, hsend.at[2], hrecv.at[2], to_y)
    loads = [pltpu.make_async_copy(s, d, lsem.at[i]) for i, (s, d) in enumerate([
        (hid.at[mine_at], x_ref.at[:, rows_at, :]),
        (wq, own_qkv.at[0]), (wk, own_qkv.at[1]), (wv, own_qkv.at[2]), (wo, own_o),
        (wg, own_g), (wu, own_u), (wd, pool.at[0:ff]),
        (hid.at[peer_at], other.at[:, rows_at, :])])]

    def piece(i, j):
        return h_all.at[4 * i + j]

    def fetch(n_sem, src, dst, k, to):
        return remote(piece(*src).at[k], piece(*dst).at[k], asend.at[n_sem], arecv.at[n_sem], to)

    y = [fetch(k, (HERE, SELF), (THERE, SELF), k, to_y) for k in range(hb)]
    x = [fetch(4 + k, (HERE, SELF), (HERE, ACROSS), k, to_x) for k in range(hb)]
    dx = [fetch(8 + k, (THERE, SELF), (THERE, ACROSS), k, to_x) for k in range(hb)]
    c_y = [fetch(12 + k, (THERE, SELF), (THERE, CORE), k, to_c) for k in range(hb)]
    c_x = [fetch(16 + k, (HERE, ACROSS), (HERE, CORNER), k, to_c) for k in range(hb)]
    c_d = [fetch(20 + k, (THERE, ACROSS), (THERE, CORNER), k, to_c) for k in range(hb)]
    c_0 = [fetch(24 + k, (HERE, SELF), (HERE, CORE), k, to_c) for k in range(hb)]
    y_a, y_b, y_c, y_d = y
    x_a, x_b, x_c, x_d = x
    dx_a, dx_b, dx_c, dx_d = dx
    c_y_a, c_y_b, c_y_c, c_y_d = c_y
    c_x_a, c_x_b, c_x_c, c_x_d = c_x
    c_d_a, c_d_b, c_d_c, c_d_d = c_d
    c_0_a, c_0_b, c_0_c, c_0_d = c_0
    fetches = y + x + dx + c_y + c_x + c_d + c_0
    first, second = (0, hb // 2), (hb // 2, hb)

    def begin(*copies):
        for copy in copies:
            copy.start()

    def arrived(*copies):
        for copy in copies:
            copy.wait_recv()

    kv_send = [remote(kvp_ref.at[m], (kc, vc)[m].at[1, mine_at], ksend.at[m], krecv.at[m], to_y) for m in range(2)]

    greet([target(i, j) for i, j in away])
    hid_a.start()
    u_copy.start()
    sends[0].start()
    for load in loads:
        load.start()

    def fill_bias(src, l, base):
        row = lax.broadcasted_iota(jnp.int32, (seq, seq), 0)
        col = lax.broadcasted_iota(jnp.int32, (seq, seq), 1)
        lines = jnp.dot(src[:, l, :], bucket_hot(src.shape[2], seq), precision=lax.Precision.HIGHEST, preferred_element_type=F32)
        for h in range(HEADS):
            line = jnp.broadcast_to(lines[h:h + 1, :], (seq, seq))
            toeplitz = pltpu.roll(line, 0, 1, stride=1, stride_axis=0)
            bias[base + h] = jnp.where(col <= row, toeplitz, -jnp.inf)

    def normed(rows, scale):
        wide = rows.astype(F32)
        inv = lax.rsqrt(jnp.mean(wide * wide, axis=-1, keepdims=True) + EPSILON)
        return (wide * inv * scale).astype(BF16)

    def heads_pass(l, side, midway=None):
        def body(s, carry):
            if midway is not None:
                pl.when(s == hb // 2)(midway)
            a = normed(x_ref[s], lna[l:l + 1, :])
            for m in range(3):
                w = own_qkv[m, l] if side == 0 else peer_qkv[l, m]
                part = jnp.dot(a, w, preferred_element_type=F32).astype(BF16)
                qkv[:, m * width:(m + 1) * width] = part
                if m > 0:
                    if side == 0:
                        kvt[l, m - 1, s] = part.T
                    elif l == 1:
                        kvp_ref[m - 1, s] = part.T
            attend_rows(qkv, bias, side * HEADS, o_all, side, s)
            if side == 1:
                out = jnp.dot(o_all[0, s], own_o[l], preferred_element_type=F32)
                out = out + jnp.dot(o_all[1, s], peer_o[l], preferred_element_type=F32)
                x_ref[s] = (x_ref[s].astype(F32) + out).astype(BF16)
            return carry
        lax.fori_loop(0, hb, body, 0)

    def ffn_chunk(gate, up, down):
        def body(r, carry):
            at = pl.ds(pl.multiple_of(r * FC, FC), FC)
            b = b_all[at, :]
            g = jnp.dot(b, gate[...], preferred_element_type=F32)
            u = jnp.dot(b, up[...], preferred_element_type=F32)
            hidden = (jax.nn.gelu(g) * u).astype(BF16)
            out = jnp.dot(hidden, down[...], preferred_element_type=F32)
            acc[at, :] = acc[at, :] + out
            return carry
        lax.fori_loop(0, 2, body, 0)

    def ffn_loop(own, steps):
        def body(c, carry):
            at = pl.ds(pl.multiple_of(c * FC, FC), FC)
            if own:
                ffn_chunk(own_g.at[:, at], own_u.at[:, at], pool.at[at, :])
            else:
                ffn_chunk(peer_g.at[c], peer_u.at[c], pool.at[pl.ds(pl.multiple_of(ff + c * FC, FC), FC), :])
            for k, step in enumerate(steps):
                pl.when(c == k)(step)
            return carry
        lax.fori_loop(0, ff // FC, body, 0)

    slot_iota = lax.broadcasted_iota(jnp.int32, (local_slots, 2 * half), 0)

    def pick(*units):
        start, end = units[0], units[-1]

        def blend(n, low, high):
            return low + n * (high - low)

        def body(step, carry):
            n, p = step // 2, lax.rem(step, 2)
            lo = blend(n, start[2][0], end[2][0])
            index_of = blend(n, 4 * start[0] + start[1], 4 * end[0] + end[1])
            tp_of = blend(n, tps[start[0]], tps[end[0]])
            ep_of = blend(n, eps[start[1]], eps[end[1]])
            h = h_all[index_of, pl.ds(lo, 2), pl.ds(pl.multiple_of(p * half, half), half), :].reshape(2 * half, d_model)
            b = normed(h, lnf[1:2, :])
            g = p * 4 + ep_of
            off = pl.multiple_of(tp_of * (hb * half) + lo * half, 2 * half)
            loc = slots_all[g, :, pl.ds(off, 2 * half)] - me * local_slots
            match = (slot_iota == loc[0:1, :]) | (slot_iota == loc[1:2, :])
            select = jnp.where(match, 1.0, 0.0).astype(BF16)
            got = jnp.dot(select, b, preferred_element_type=F32).astype(BF16)
            for e in range(n_exp):
                at = pl.ds(pl.multiple_of(e * local_slots + g * capacity, capacity), capacity)
                pool[at, :] = pool[at, :] + got[e * capacity:(e + 1) * capacity, :]
            return carry
        lax.fori_loop(0, 2 * len(units), body, 0)

    w0 = [('w', 0, m) for m in range(3)]
    w1 = [('w', 1, m) for m in range(3)]
    w1_a, w1_b, w1_c = w1
    o0, o1 = ('o', 0, 0), ('o', 1, 0)
    g = [('g', c, 0) for c in range(3)]
    u = [('u', c, 0) for c in range(3)]
    d = [('d', c, 0) for c in range(3)]
    g_a, g_b, g_c = g
    u_a, u_b, u_c = u
    d_a, d_b, d_c = d

    for k in range(ids.shape[0]):
        ids_row[:, k * half:(k + 1) * half] = ids[k]
    experts = lax.broadcasted_iota(jnp.int32, (64, tokens), 0)
    hot = [experts == ids_row[c:c + 1, :] for c in range(2)]
    ones = [jnp.where(h, 1.0, 0.0) for h in hot]
    earlier = jnp.where(lax.broadcasted_iota(jnp.int32, (tokens, tokens), 0)
                        < lax.broadcasted_iota(jnp.int32, (tokens, tokens), 1), 1.0, 0.0).astype(BF16)
    before = [jnp.dot(o.astype(BF16), earlier, preferred_element_type=F32) for o in ones]
    before[1] = before[1] + jnp.sum(ones[0], axis=1, keepdims=True)
    for c in range(2):
        pos = jnp.sum(jnp.where(hot[c], before[c], 0.0), axis=0, keepdims=True).astype(jnp.int32)
        slots_all[me, c:c + 1, :] = jnp.where(pos < capacity, ids_row[c:c + 1, :] * capacity + pos, -1)
    slot_sends = [remote(slots_all.at[me], slots_all.at[me], ssend.at[4 * i + j], srecv.at[4 * i + j], target(i, j))
                  for i, j in away]
    for copy in slot_sends:
        copy.start()
    for c in range(2):
        slot = slots_all[me, c:c + 1, :]
        expert = lax.shift_right_arithmetic(slot, 6)
        key = lax.bitwise_and(expert, 7) * local_slots + lax.shift_right_arithmetic(expert, 3) * capacity + lax.bitwise_and(slot, 63)
        key = jnp.where(slot < 0, -1, key).astype(F32)
        aux[:, c * 8:(c + 1) * 8] = jnp.broadcast_to(key, (8, tokens)).T
        aux[:, 16 + c * 8:24 + c * 8] = jnp.broadcast_to(ids_row[c:c + 1, :].astype(F32), (8, tokens)).T

    fill_bias(table_own, 0, 0)
    u_copy.wait_recv()
    fill_bias(table_peer, 0, HEADS)
    loads[0].wait()
    hid_a.wait_recv()
    for copy in sends[1:WINDOW]:
        copy.start()
    for load in loads[1:4]:
        load.wait()
    heads_pass(0, 0)
    pass_on(*w0, o0)
    pass_core(*w0)
    pass_on(g_a)
    pass_core(o0)
    complete(*w0, o0)
    pass_on(u_a)
    loads[4].wait()

    def midway():
        pass_on(d_a)
        pass_core(g_a)
    heads_pass(0, 1, midway)
    pass_core(u_a)
    pass_on(g_b)

    def norm_rows(s, carry):
        b_all[pl.ds(pl.multiple_of(s * seq, seq), seq), :] = normed(x_ref[s], lnf[0:1, :])
        return carry
    lax.fori_loop(0, hb, norm_rows, 0)
    for load in loads[5:8]:
        load.wait()
    acc[...] = jnp.zeros_like(acc)

    def own_a():
        pass_on(u_b)
        pass_core(d_a)

    def own_b():
        pass_core(g_b)
        pass_on(d_b)
        pass_core(u_b)

    def own_c():
        pass_on(g_c)
        complete(g_a, u_a, d_a)
    ffn_loop(True, [own_a, own_b, own_c])

    def peer_a():
        pass_core(d_b, g_c)
        pass_on(u_c)
        complete(g_b, u_b, d_b)

    def peer_b():
        fill_bias(table_own, 1, 0)
        pass_on(d_c)
        pass_core(u_c)
        fill_bias(table_peer, 1, HEADS)
        pass_on(w1_a)
        pass_core(d_c)
        complete(g_c, u_c, d_c)
    ffn_loop(False, [peer_a, peer_b])

    def add_rows(s, carry):
        x_ref[s] = (x_ref[s].astype(F32) + acc[pl.ds(pl.multiple_of(s * seq, seq), seq), :]).astype(BF16)
        return carry
    lax.fori_loop(0, hb, add_rows, 0)

    pass_on(w1_b, w1_c)
    pass_core(w1_a)

    def own_midway():
        pass_on(o1)
        pass_core(w1_b, w1_c)
    heads_pass(1, 0, own_midway)
    pass_core(o1)
    complete(*w1, o1)
    for item in d:
        x_copy(item).wait_send()
        c_copy(item).wait_send()
        d_copy(item).wait_send()
    stores = [pltpu.make_async_copy(kvt.at[l, m], (kc, vc)[m].at[l, mine_at], osem.at[2 * l + m])
              for l in range(2) for m in range(2)]
    begin(*stores)
    heads_pass(1, 1, lambda: begin(y_a, x_a, y_b, x_b, c_0_a, c_0_b))
    begin(c_0_c, c_0_d)

    pool[...] = jnp.zeros_like(pool)
    for copy in slot_sends:
        copy.wait_recv()
    pick((HERE, SELF, first), (HERE, SELF, second))
    loads[8].wait()
    hid_b.wait_recv()
    stores[0].wait()
    stores[1].wait()

    def other_rows(s, carry):
        a = normed(other[s], lna[0:1, :])
        for m in range(2):
            kvt[0, m, s] = jnp.dot(a, own_qkv[m + 1, 0], preferred_element_type=F32).astype(BF16).T
        return carry
    lax.fori_loop(0, hb, other_rows, 0)
    more = [pltpu.make_async_copy(kvt.at[0, m], (kc, vc)[m].at[0, peer_at], osem.at[4 + m]) for m in range(2)]
    begin(*more)

    arrived(*c_0)
    pick((HERE, CORE, first), (HERE, CORE, second))
    arrived(x_a)
    begin(x_c, c_x_a)
    arrived(x_b)
    begin(x_d, c_x_b)
    arrived(y_a)
    begin(y_c, dx_a, c_y_a)
    arrived(y_b)
    begin(y_d, dx_b, c_y_b)
    pick((HERE, ACROSS, first), (THERE, SELF, first))
    arrived(c_x_a, c_x_b, c_y_a, c_y_b)
    pick((HERE, CORNER, first), (THERE, CORE, first))
    arrived(y_c)
    begin(dx_c, kv_send[0], c_y_c)
    arrived(y_d)
    begin(dx_d, kv_send[1], c_y_d)
    arrived(c_y_c, c_y_d)
    pick((THERE, SELF, second), (THERE, CORE, second))

    pos_at = pl.ds(pl.multiple_of(tp * half, half), half)
    for i in range(2):
        at = pl.ds(pl.multiple_of(tps[i] * (hb * half), hb * half), hb * half)
        h = piece(i, 0)[:, pos_at, :].reshape(hb * half, d_model)
        own_h[at, :] = h
        logits = lax.dot_general(normed(h, lnf[1:2, :]).astype(F32), w_router[...], (((1,), (1,)), ((), ())),
                                 precision=lax.Precision.HIGHEST, preferred_element_type=F32)
        ex = jnp.exp(logits - jnp.max(logits, axis=1, keepdims=True))
        probs = ex / jnp.sum(ex, axis=1, keepdims=True)
        lanes = lax.broadcasted_iota(jnp.int32, probs.shape, 1).astype(F32)
        picked = [jnp.sum(jnp.where(lanes == aux[at, 16 + c * 8:17 + c * 8], probs, 0.0), axis=1, keepdims=True) for c in range(2)]
        denom = picked[0] + picked[1]
        for c in range(2):
            aux[at, 32 + c:33 + c] = picked[c] / denom

    arrived(x_c)
    begin(c_x_c)
    arrived(x_d)
    begin(c_x_d)
    arrived(c_x_c, c_x_d)
    pick((HERE, ACROSS, second), (HERE, CORNER, second))
    arrived(dx_a)
    begin(c_d_a)
    arrived(dx_b)
    begin(c_d_b)
    arrived(c_d_a, c_d_b)
    pick((THERE, ACROSS, first), (THERE, CORNER, first))
    arrived(dx_c)
    begin(c_d_c)
    arrived(dx_d)
    begin(c_d_d)
    pick((THERE, ACROSS, second))
    arrived(c_d_c, c_d_d)
    pick((THERE, CORNER, second))

    out = [pltpu.make_async_copy(pool.at[e * local_slots:(e + 1) * local_slots], rows_out.at[e], lsem.at[e]) for e in range(n_exp)]
    begin(*out)
    for copy in out + stores[2:] + more:
        copy.wait()
    for copy in [hid_a, hid_b, u_copy] + fetches + slot_sends:
        copy.wait_send()
    for copy in kv_send:
        copy.wait()
    for item in items:
        y_copy(item).wait_send()
        if item not in d:
            x_copy(item).wait_send()
            c_copy(item).wait_send()
            d_copy(item).wait_send()


def dense_layers(hid, lna, lnf, wq, wk, wv, wo, wg, wu, wd, bias_table, ids, w_router):
    nb, npos, d_model = hid.shape
    hb, seq = nb // 2, 2 * npos
    tokens = nb * npos
    width = HEADS * 64
    ff = wg.shape[1]
    any_spec = pl.BlockSpec(memory_space=pl.ANY)
    vmem = pl.BlockSpec(memory_space=pltpu.VMEM)
    n_items = 17
    dma = pltpu.SemaphoreType.DMA
    slots = LOCAL_EXPERTS * CAPACITY
    return pl.pallas_call(
        dense_kernel,
        in_specs=[any_spec, vmem, vmem] + [any_spec] * 7 + [vmem] * 3,
        out_specs=[any_spec, vmem, vmem, any_spec, any_spec],
        out_shape=[jax.ShapeDtypeStruct((LOCAL_EXPERTS, slots, d_model), BF16),
                   jax.ShapeDtypeStruct((tokens, 128), F32),
                   jax.ShapeDtypeStruct((tokens, d_model), BF16),
                   jax.ShapeDtypeStruct((2, nb, width, seq), BF16),
                   jax.ShapeDtypeStruct((2, nb, width, seq), BF16)],
        scratch_shapes=[
            pltpu.VMEM((3, 2, d_model, width), BF16), pltpu.VMEM((2, width, d_model), BF16),
            pltpu.VMEM((d_model, ff), BF16), pltpu.VMEM((d_model, ff), BF16),
            pltpu.VMEM((2, 3, d_model, width), BF16), pltpu.VMEM((2, width, d_model), BF16),
            pltpu.VMEM((3, d_model, FC), BF16), pltpu.VMEM((3, d_model, FC), BF16),
            pltpu.VMEM((LOCAL_EXPERTS * slots, d_model), BF16),
            pltpu.VMEM(bias_table.shape, F32), pltpu.VMEM((2 * HEADS, seq, seq), F32),
            pltpu.VMEM((seq, 3 * width), BF16), pltpu.VMEM((2, hb, seq, width), BF16),
            pltpu.VMEM((hb * seq, d_model), BF16), pltpu.VMEM((hb * seq, d_model), F32),
            pltpu.VMEM((2, 2, hb, width, seq), BF16), pltpu.VMEM((hb, seq, d_model), BF16),
            pltpu.VMEM((2, hb, width, seq), BF16), pltpu.VMEM((8, hb, seq, d_model), BF16), pltpu.VMEM((8, 2, tokens), jnp.int32), pltpu.VMEM((2, tokens), jnp.int32),
        ] + [dma((n_items,))] * 8 + [dma((3,)), dma((3,)), dma((9,)), dma((6,)),
                                     dma((28,)), dma((28,)), dma((8,)), dma((8,)), dma((2,)), dma((2,))],
        compiler_params=pltpu.CompilerParams(collective_id=0, has_side_effects=True, vmem_limit_bytes=65470 * 1024),
        name="dense_layers",
    )(hid, lna, lnf, wq, wk, wv, wo, wg, wu, wd, bias_table, ids, w_router)


def moe_kernel(rows_in, aux, own_h, w_in, w_out,
               out_ref,
               rows, res, ret, win, wout, acc, total,
               rsend, rrecv, wsem, isem):
    tp, ep, to_y, to_x, to_c = swap_targets()
    n_exp, local_slots, d_model = rows.shape
    capacity = local_slots // 8
    tokens = own_h.shape[0]
    chunk = win.shape[2]
    n_chunks = w_in.shape[2] // chunk
    eps = [ep, to_c['ep'], to_x['ep'], lax.rem(to_c['ep'] + 2, 4)]
    tps = [tp, 1 - tp]
    me = tp * 4 + ep
    away = [(i, j) for i in (1, 0) for j in (2, 3, 0, 1) if (i, j) != (0, 0)]

    def target(i, j):
        return {'tp': tps[i], 'ep': eps[j]}

    def remote(src, dst, send, recv, to):
        return pltpu.make_async_remote_copy(src_ref=src, dst_ref=dst, send_sem=send, recv_sem=recv,
                                            device_id=to, device_id_type=MESH)

    def weight_copies(e, c):
        at = pl.ds(c * chunk, chunk)
        return (pltpu.make_async_copy(w_in.at[e, :, at], win.at[c], wsem.at[0, c]),
                pltpu.make_async_copy(w_out.at[e, at, :], wout.at[c], wsem.at[1, c]))

    def row_copy(e):
        return pltpu.make_async_copy(rows_in.at[e], rows.at[e], isem.at[e])

    row_copy(0).start()
    for c in range(n_chunks):
        for copy in weight_copies(0, c):
            copy.start()
    for e in range(1, n_exp):
        row_copy(e).start()
    greet([target(i, j) for i, j in away])
    total[...] = jnp.zeros_like(total)

    def returns(e):
        return [remote(res.at[e, tps[i] * 4 + eps[j]], ret.at[e, me], rsend.at[4 * i + j, e], rrecv.at[4 * i + j, e], target(i, j))
                for i, j in away]

    def combine(e):
        for copy in returns(e):
            copy.wait_recv()
        block = 256
        columns = lax.broadcasted_iota(jnp.int32, (block, local_slots), 1).astype(F32)
        table = ret[e].reshape(local_slots, d_model)

        def body(r, carry):
            at = pl.ds(pl.multiple_of(r * block, block), block)
            add = total[at, :]
            for c in range(2):
                want = aux[at, c * 8:c * 8 + 1] - (e * local_slots).astype(F32)
                select = jnp.where(columns == want, 1.0, 0.0).astype(BF16)
                add = add + aux[at, 32 + c:33 + c] * jnp.dot(select, table, preferred_element_type=F32)
            total[at, :] = add
            return carry
        lax.fori_loop(0, tokens // block, body, 0)

    lag = 3

    def expert(e, carry):
        row_copy(e).wait()
        table = rows[e]
        for c in range(n_chunks):
            for copy in weight_copies(e, c):
                copy.wait()
            up = jnp.dot(table, win[c], preferred_element_type=F32)
            out = jnp.dot(jax.nn.gelu(up).astype(BF16), wout[c], preferred_element_type=F32)
            if c == 0:
                acc[...] = out
            elif c < n_chunks - 1:
                acc[...] = acc[...] + out
            else:
                res[e] = (acc[...] + out).astype(BF16).reshape(8, capacity, d_model)

            @pl.when(e < n_exp - 1)
            def _():
                for copy in weight_copies(e + 1, c):
                    copy.start()
        for copy in returns(e):
            copy.start()
        ret[e, me] = res[e, me]

        @pl.when(e >= lag)
        def _():
            combine(e - lag)
        return carry
    lax.fori_loop(0, n_exp, expert, 0)

    def last(e, carry):
        combine(e)
        return carry
    lax.fori_loop(n_exp - lag, n_exp, last, 0)
    out_ref[...] = (own_h[...].astype(F32) + total[...]).astype(BF16).reshape(out_ref.shape)


    def drain(e, carry):
        for copy in returns(e):
            copy.wait_send()
        return carry
    lax.fori_loop(0, n_exp, drain, 0)


def moe_layer(rows, aux, own_h, w_in, w_out, out_shape):
    n_exp, slots, d_model = rows.shape
    tokens = own_h.shape[0]
    ff = w_in.shape[2]
    capacity = slots // 8
    chunk = 768
    n_chunks = ff // chunk
    vmem = pl.BlockSpec(memory_space=pltpu.VMEM)
    any_spec = pl.BlockSpec(memory_space=pl.ANY)
    dma = pltpu.SemaphoreType.DMA
    slot_rows = pltpu.VMEM((n_exp, 8, capacity, d_model), BF16)
    return pl.pallas_call(
        moe_kernel,
        in_specs=[any_spec, vmem, vmem] + [any_spec] * 2,
        out_specs=vmem,
        out_shape=jax.ShapeDtypeStruct(out_shape, BF16),
        scratch_shapes=[
            pltpu.VMEM((n_exp, slots, d_model), BF16), slot_rows, slot_rows,
            pltpu.VMEM((n_chunks, d_model, chunk), BF16), pltpu.VMEM((n_chunks, chunk, d_model), BF16),
            pltpu.VMEM((slots, d_model), F32), pltpu.VMEM((tokens, d_model), F32),
            dma((8, n_exp)), dma((8, n_exp)), dma((2, n_chunks)), dma((n_exp,)),
        ],
        compiler_params=pltpu.CompilerParams(collective_id=1, has_side_effects=True, vmem_limit_bytes=62 * 1024 * 1024),
        name="moe_layer",
    )(rows, aux, own_h, w_in, w_out)


def solution(mesh):
    act_spec = P(('dp', 'ep'), 'tp', None)
    col_spec = P(None, None, 'tp')
    row_spec = P(None, 'tp', None)
    expert_spec = P(('tp', 'ep'), None, None)
    cache_spec = P(None, ('dp', 'ep'), 'tp', None, None)
    in_specs = (act_spec, P(), P(), col_spec, col_spec, col_spec, row_spec, row_spec,
                P(None, 'tp'), P(None, 'tp'), P('tp', None), P(), expert_spec, expert_spec, act_spec)

    def device_fn(hidden_in, ln_attn, ln_ffn, w_query, w_key, w_value, w_out, bias_table, w_gate, w_up, w_down, w_router, expert_in, expert_out, expert_ids):
        nb, npos, d_model = hidden_in.shape
        rows, aux, own_h, k_all, v_all = dense_layers(
            hidden_in, ln_attn, ln_ffn, w_query, w_key, w_value, w_out, w_gate, w_up, w_down,
            jnp.swapaxes(bias_table, 0, 1), jnp.swapaxes(expert_ids, 1, 2), w_router.T)
        hidden = moe_layer(rows, aux, own_h, expert_in, expert_out, hidden_in.shape)
        caches = [jnp.swapaxes(full.reshape(2, nb, -1, 64, 2 * npos), 3, 4) for full in (k_all, v_all)]
        return hidden, caches[0], caches[1]

    return jax.shard_map(device_fn, mesh=mesh, in_specs=in_specs, out_specs=(act_spec, cache_spec, cache_spec), check_vma=False)
```

profile of v0, /device:TPU:0, one launch (start us, length us, event | category | flops | bytes accessed | tf_op | source)
XLA Modules:
  0.0 278.7 jit_solution(13145181275045369463)
XLA Ops:
  0.6 185.6 %dense_layers.1 = (bf16[8,512,768]{2,1,0:T(8,128)(2,1)}, f32[1024,128]{1,0:T(8,128)}, bf16[1024,768]{1,0:T(8,128)(2,1)}, bf16[2,8,384,256]{3,2,1,0:T(8,128)(2,1)}, bf16[2,8,384,256]{3,2,1,0:T(8,128)(2,1)}) custom-call(bf16[8,128,768]{2,1,0:T(8,128)(2,1)} %hid.1, f32[2,768]{1,0:T(2,128)} %lna.1, f32[2,768]{1,0:T(2,128)} %lnf.1, bf16[2,768,384]{2,1,0:T(8,128)(2,1)} %wq.1, ...), custom_call_target="tpu_custom_call" | custom-call | tf_op jit(solution)/shard_map/dense_layers/pallas_call | solution.py:533
  186.2 85.0 %moe_layer.1 = bf16[8,128,768]{2,1,0:T(8,128)(2,1)} custom-call(bf16[8,512,768]{2,1,0:T(8,128)(2,1)} %get-tuple-element.8.rows_in, f32[1024,128]{1,0:T(8,128)} %get-tuple-element.9.aux, bf16[1024,768]{1,0:T(8,128)(2,1)} %get-tuple-element.10.own_h, bf16[8,768,3072]{2,1,0:T(8,128)(2,1)} %w_in.1, bf16[8,3072,768]{2,1,0:T(8,128)(2,1)} %w_out.1), custom_call_target="tpu_custom_call" | custom-call | tf_op jit(solution)/shard_map/moe_layer/pallas_call | solution.py:677
  271.2 0.0 copy-start.1
  271.2 2.8 %copy.21 = bf16[8,128,768]{2,1,0:T(8,128)(2,1)} copy(bf16[8,128,768]{2,1,0:T(8,128)(2,1)} %moe_layer.1) | data formatting | bytes 3145728
  274.0 0.0 copy-done.1
  274.0 0.0 copy-start
  274.0 1.7 copy.22
  275.7 1.4 copy-done
  277.0 1.7 copy.23
Async XLA Ops:
  271.2 2.8 %copy-start.1 = (bf16[2,8,384,256]{3,2,1,0:T(8,128)(2,1)S(1)}, bf16[2,8,384,256]{3,2,1,0:T(8,128)(2,1)}, u32[]{:S(2)}) copy-start(bf16[2,8,384,256]{3,2,1,0:T(8,128)(2,1)} %get-tuple-element.11) | copy-start | bytes 9437188
  274.0 3.0 %copy-start = (bf16[2,8,384,256]{3,2,1,0:T(8,128)(2,1)S(1)}, bf16[2,8,384,256]{3,2,1,0:T(8,128)(2,1)}, u32[]{:S(2)}) copy-start(bf16[2,8,384,256]{3,2,1,0:T(8,128)(2,1)} %get-tuple-element.12) | copy-start | bytes 9437188
where the time goes:
time: 279 us
  Pallas kernels  271 us (97%)
  local copies, waits for them, and re-layouts  7.49 us (3%)
    pallas_call x1, Pallas kernels, dense_layers(): pl.pallas_call(dense_kernel, in_specs=[any_spec, vmem, vmem] + [any_spec]...  186 us
    pallas_call x1, Pallas kernels, moe_layer(): pl.pallas_call(moe_kernel, in_specs=[any_spec, vmem, vmem] + [any_spec] *...  85 us
    unnamed x7, local copies, waits for them, and re-layouts  7.49 us

commit v1 on v0

--- a/solution.py
+++ b/solution.py
@@ -235,10 +235,10 @@
         inv = lax.rsqrt(jnp.mean(wide * wide, axis=-1, keepdims=True) + EPSILON)
         return (wide * inv * scale).astype(BF16)
 
-    def heads_pass(l, side, midway=None):
+    def heads_pass(l, side, midway):
         def body(s, carry):
-            if midway is not None:
-                pl.when(s == hb // 2)(midway)
+            for k, step in midway.items():
+                pl.when(s == k)(step)
             a = normed(x_ref[s], lna[l:l + 1, :])
             for m in range(3):
                 w = own_qkv[m, l] if side == 0 else peer_qkv[l, m]
@@ -353,7 +353,7 @@
         copy.start()
     for load in loads[1:4]:
         load.wait()
-    heads_pass(0, 0)
+    heads_pass(0, 0, {})
     pass_on(*w0, o0)
     pass_core(*w0)
     pass_on(g_a)
@@ -365,7 +365,7 @@
     def midway():
         pass_on(d_a)
         pass_core(g_a)
-    heads_pass(0, 1, midway)
+    heads_pass(0, 1, {hb // 2: midway})
     pass_core(u_a)
     pass_on(g_b)
 
@@ -417,7 +417,7 @@
     def own_midway():
         pass_on(o1)
         pass_core(w1_b, w1_c)
-    heads_pass(1, 0, own_midway)
+    heads_pass(1, 0, {hb // 2: own_midway})
     pass_core(o1)
     complete(*w1, o1)
     for item in d:
@@ -427,8 +427,9 @@
     stores = [pltpu.make_async_copy(kvt.at[l, m], (kc, vc)[m].at[l, mine_at], osem.at[2 * l + m])
               for l in range(2) for m in range(2)]
     begin(*stores)
-    heads_pass(1, 1, lambda: begin(y_a, x_a, y_b, x_b, c_0_a, c_0_b))
-    begin(c_0_c, c_0_d)
+    ready = [lambda: begin(y_a, x_a, c_0_a), lambda: begin(y_b, x_b, c_0_b), lambda: begin(y_c, x_c, c_0_c)]
+    heads_pass(1, 1, {k + 1: step for k, step in enumerate(ready)})
+    begin(c_0_d)
 
     pool[...] = jnp.zeros_like(pool)
     for copy in slot_sends:
@@ -451,20 +452,20 @@
     arrived(*c_0)
     pick((HERE, CORE, first), (HERE, CORE, second))
     arrived(x_a)
-    begin(x_c, c_x_a)
+    begin(x_d, c_x_a)
     arrived(x_b)
-    begin(x_d, c_x_b)
+    begin(c_x_b)
     arrived(y_a)
-    begin(y_c, dx_a, c_y_a)
+    begin(y_d, dx_a, c_y_a)
     arrived(y_b)
-    begin(y_d, dx_b, c_y_b)
+    begin(dx_b, kv_send[0], c_y_b)
     pick((HERE, ACROSS, first), (THERE, SELF, first))
     arrived(c_x_a, c_x_b, c_y_a, c_y_b)
     pick((HERE, CORNER, first), (THERE, CORE, first))
     arrived(y_c)
-    begin(dx_c, kv_send[0], c_y_c)
+    begin(dx_c, kv_send[1], c_y_c)
     arrived(y_d)
-    begin(dx_d, kv_send[1], c_y_d)
+    begin(dx_d, c_y_d)
     arrived(c_y_c, c_y_d)
     pick((THERE, SELF, second), (THERE, CORE, second))
 
@@ -618,6 +619,26 @@
             return carry
         lax.fori_loop(0, tokens // block, body, 0)
 
+    def first_expert():
+        part = rows.shape[1] // 2
+        for i in (1, 0):
+            at = pl.ds(pl.multiple_of(tps[i] * part, part), part)
+            for c in range(n_chunks):
+                if i == 1:
+                    for copy in weight_copies(0, c):
+                        copy.wait()
+                up = jnp.dot(rows[0, at, :], win[c], preferred_element_type=F32)
+                out = jnp.dot(jax.nn.gelu(up).astype(BF16), wout[c], preferred_element_type=F32)
+                acc[at, :] = out if c == 0 else acc[at, :] + out
+                if i == 0:
+                    for copy in weight_copies(1, c):
+                        copy.start()
+            res[0, pl.ds(tps[i] * 4, 4)] = acc[at, :].astype(BF16).reshape(4, capacity, d_model)
+            for to, copy in zip(away, returns(0)):
+                if to[0] == i:
+                    copy.start()
+        ret[0, me] = res[0, me]
+
     lag = 3
 
     def expert(e, carry):
@@ -647,7 +668,9 @@
         def _():
             combine(e - lag)
         return carry
-    lax.fori_loop(0, n_exp, expert, 0)
+    row_copy(0).wait()
+    first_expert()
+    lax.fori_loop(1, n_exp, expert, 0)
 
     def last(e, carry):
         combine(e)

time: 279 us -> 276 us (0.989)
  Pallas kernels: 271 us -> 268 us
where the time goes in v1:
time: 276 us
  Pallas kernels  268 us (97%)
  local copies, waits for them, and re-layouts  7.49 us (3%)
    pallas_call x1, Pallas kernels, dense_layers(): pl.pallas_call(dense_kernel, in_specs=[any_spec, vmem, vmem] + [any_spec]...  184 us
    pallas_call x1, Pallas kernels, moe_layer(): pl.pallas_call(moe_kernel, in_specs=[any_spec, vmem, vmem] + [any_spec] *...  84.1 us
    unnamed x7, local copies, waits for them, and re-layouts  7.49 us

profile of v1, /device:TPU:0, one launch (start us, length us, event | category | flops | bytes accessed | tf_op | source)
XLA Modules:
  0.0 275.9 jit_solution(8918086058265555538)
XLA Ops:
  0.6 183.7 %dense_layers.1 = (bf16[8,512,768]{2,1,0:T(8,128)(2,1)}, f32[1024,128]{1,0:T(8,128)}, bf16[1024,768]{1,0:T(8,128)(2,1)}, bf16[2,8,384,256]{3,2,1,0:T(8,128)(2,1)}, bf16[2,8,384,256]{3,2,1,0:T(8,128)(2,1)}) custom-call(bf16[8,128,768]{2,1,0:T(8,128)(2,1)} %hid.1, f32[2,768]{1,0:T(2,128)} %lna.1, f32[2,768]{1,0:T(2,128)} %lnf.1, bf16[2,768,384]{2,1,0:T(8,128)(2,1)} %wq.1, ...), custom_call_target="tpu_custom_call" | custom-call | tf_op jit(solution)/shard_map/dense_layers/pallas_call | solution.py:534
  184.4 84.1 %moe_layer.1 = bf16[8,128,768]{2,1,0:T(8,128)(2,1)} custom-call(bf16[8,512,768]{2,1,0:T(8,128)(2,1)} %get-tuple-element.8.rows_in, f32[1024,128]{1,0:T(8,128)} %get-tuple-element.9.aux, bf16[1024,768]{1,0:T(8,128)(2,1)} %get-tuple-element.10.own_h, bf16[8,768,3072]{2,1,0:T(8,128)(2,1)} %w_in.1, bf16[8,3072,768]{2,1,0:T(8,128)(2,1)} %w_out.1), custom_call_target="tpu_custom_call" | custom-call | tf_op jit(solution)/shard_map/moe_layer/pallas_call | solution.py:700
  268.4 0.0 copy-start.1
  268.4 2.8 %copy.21 = bf16[8,128,768]{2,1,0:T(8,128)(2,1)} copy(bf16[8,128,768]{2,1,0:T(8,128)(2,1)} %moe_layer.1) | data formatting | bytes 3145728
  271.2 0.0 copy-done.1
  271.2 0.0 copy-start
  271.2 1.7 copy.22
  272.9 1.4 copy-done
  274.3 1.7 copy.23
Async XLA Ops:
  268.4 2.8 %copy-start.1 = (bf16[2,8,384,256]{3,2,1,0:T(8,128)(2,1)S(1)}, bf16[2,8,384,256]{3,2,1,0:T(8,128)(2,1)}, u32[]{:S(2)}) copy-start(bf16[2,8,384,256]{3,2,1,0:T(8,128)(2,1)} %get-tuple-element.11) | copy-start | bytes 9437188
  271.2 3.0 %copy-start = (bf16[2,8,384,256]{3,2,1,0:T(8,128)(2,1)S(1)}, bf16[2,8,384,256]{3,2,1,0:T(8,128)(2,1)}, u32[]{:S(2)}) copy-start(bf16[2,8,384,256]{3,2,1,0:T(8,128)(2,1)} %get-tuple-element.12) | copy-start | bytes 9437188
